TPU v7x, 32 devices: a whole 2x2x4 slice. The times are simulated.
32 devices in a mesh: replica: 4 (over x, core), fsdp: 8 (over z, y).
Axes of the slice: x: 2, y: 2, z: 4, core: 2. Of those that a mesh axis runs over, the one named last changes fastest.
Arguments:
- deltas: bfloat16 [4, 2, 2048, 16384], P('replica', None, 'fsdp'), may hold values from -3 to 3
- master: float32 [2, 2048, 16384], P(None, 'replica', 'fsdp'), may hold values from -3 to 3
- momentum: float32 [2, 2048, 16384], P(None, 'replica', 'fsdp'), may hold values from -2 to 2
Outputs:
- master_out: float32 [2, 2048, 16384], P(None, 'replica', 'fsdp')
- momentum_out: float32 [2, 2048, 16384], P(None, 'replica', 'fsdp')
- params_out: bfloat16 [2, 2048, 16384], P(None, 'fsdp')
All inputs are finite; a program needn't handle non-finite values.
Results may differ from a plain program's by a relative error of at most 0.008.
Values may be sent and summed in bfloat16 or wider, within the bound.
A program may use at most 128 MiB of HBM per device.

v0:
```python
import jax
import jax.numpy as jnp
from jax import lax
from jax.sharding import PartitionSpec as P


def on_device(deltas, master, momentum):
    local = deltas[0]
    groups = lax.axis_size("replica")
    moved = lax.all_to_all(local, "fsdp", split_axis=2, concat_axis=1, tiled=True)
    summed = lax.psum_scatter(
        moved.astype(jnp.float32).astype(jnp.bfloat16), "replica", scatter_dimension=1, tiled=True
    ).astype(jnp.float32)
    outer = summed / groups
    velocity = 0.9 * momentum + outer
    updated = master - 0.7 * (outer + 0.9 * velocity)
    rounded = updated.astype(jnp.bfloat16)
    copies = lax.all_gather(rounded, "replica", axis=1, tiled=True)
    spread = lax.all_to_all(copies, "fsdp", split_axis=1, concat_axis=2, tiled=True)
    return (updated, velocity, spread)


def solution(mesh):
    return jax.shard_map(
        on_device,
        mesh=mesh,
        in_specs=(
            P("replica", None, "fsdp", None),
            P(None, "replica", "fsdp"),
            P(None, "replica", "fsdp"),
        ),
        out_specs=(P(None, "replica", "fsdp"), P(None, "replica", "fsdp"), P(None, "fsdp", None)),
        check_vma=False,
    )
```

profile of v0, /device:TPU:0, one launch (start us, length us, event | category | flops | bytes accessed | tf_op | source)
XLA Modules:
  0.0 1325.4 jit_solution(8873194051052167290)
XLA Ops:
  7.2 0.0 all-reduce.3.cloned.1.call-start
  7.2 40.8 %copy.22 = bf16[1,2,256,16384]{2,1,3,0:T(2,128)(2,1)} copy(bf16[1,2,256,16384]{3,2,1,0:T(8,128)(2,1)} %param.3) | data formatting | bytes 33554432 | tf_op args[0]
  48.0 372.0 %all_to_all.36 = bf16[2,256,16384]{1,0,2:T(2,128)(2,1)} all-to-all(bf16[2,256,16384]{1,0,2:T(2,128)(2,1)} %bitcast.14), channel_id=1, replica_groups=mesh['replica'=4,'fsdp'=8] {'fsdp'}, dimensions={2} | all-to-all | bytes 33554432 | tf_op jit(solution)/shard_map/all_to_all | solution.py:10
  420.0 60.3 %copy.23 = bf16[2,8,256,2048]{3,0,2,1:T(2,128)(2,1)} copy(bf16[2,8,256,2048]{2,0,3,1:T(2,128)(2,1)} %bitcast.12) | data formatting | bytes 33554432 | tf_op jit(solution)/shard_map/all_to_all | solution.py:10
  480.3 0.0 copy-start
  480.3 0.0 all-reduce.3.cloned.1.call-update
  480.3 0.0 all-gather.2.cloned.1.call-start
  480.4 0.6 copy-done
  481.0 0.6 dynamic-slice
  482.2 285.7 %all-reduce.3.cloned.1.call-done = bf16[2,2048,2048]{2,0,1:T(2,128)(2,1)} async-done(((bf16[2,2048,2048]{2,0,1:T(2,128)(2,1)}), bf16[2,2048,2048]{2,0,1:T(2,128)(2,1)}) %all-reduce.3.cloned.1.call-update) | async-done | bytes 16777232
  767.9 5.1 constant_dynamic-slice_fusion
  773.0 13.9 %fusion = (bf16[2,512,2048]{2,1,0:T(8,128)(2,1)}, f32[2,512,2048]{2,1,0:T(8,128)}, f32[2,512,2048]{2,1,0:T(8,128)}) fusion(f32[2,512,2048]{2,1,0:T(8,128)} %param.4, bf16[2,512,2048]{2,0,1:T(2,128)(2,1)S(1)} %constant_dynamic-slice_fusion, f32[2,512,2048]{2,1,0:T(8,128)} %param.5), kind=kLoop, calls=%fused_computation.4 | loop fusion | flops 18874368 | bytes 41943040 | tf_op jit(solution)/shard_map/convert_element_type | solution.py:17
  786.9 8.4 copy.25
  795.3 0.0 all-gather.2.cloned.1.call-update
  795.3 106.1 %all-gather.2.cloned.1.call-done = bf16[2,2048,2048]{2,0,1:T(2,128)(2,1)} async-done(((bf16[2,512,2048]{2,0,1:T(2,128)(2,1)}), bf16[2,2048,2048]{2,0,1:T(2,128)(2,1)}) %all-gather.2.cloned.1.call-update) | async-done | bytes 16777232 | tf_op jit(solution)/shard_map/all_gather | solution.py:18
  901.4 368.7 %all_to_all.37 = bf16[2,2048,2048]{2,0,1:T(2,128)(2,1)S(1)} all-to-all(bf16[2,2048,2048]{2,0,1:T(2,128)(2,1)} %all-gather.2.cloned.1.call-done), channel_id=1, replica_groups=mesh['replica'=4,'fsdp'=8] {'fsdp'}, dimensions={1} | all-to-all | bytes 33554432 | tf_op jit(solution)/shard_map/all_to_all | solution.py:19
  1270.1 22.9 %copy.26 = bf16[2,256,8,2048]{3,2,1,0:T(8,128)(2,1)} copy(bf16[2,256,8,2048]{3,0,1,2:T(2,128)(2,1)S(1)} %bitcast.13) | data formatting | bytes 33554432 | tf_op jit(solution)/shard_map/all_to_all | solution.py:19
  1293.0 25.5 %all_to_all.33 = bf16[2,256,16384]{2,1,0:T(8,128)(2,1)} reshape(bf16[2,256,8,2048]{3,2,1,0:T(8,128)(2,1)} %copy.26) | data formatting | bytes 33554432 | tf_op jit(solution)/shard_map/all_to_all | solution.py:19
Async XLA Ops:
  7.2 760.7 %all-reduce.3.cloned.1.call-start = ((), (), s32[]{:S(2)}) async-start(), calls=%async_computation.3 | async-start | bytes 33554432
  480.3 0.7 copy-start
  480.3 421.1 %all-gather.2.cloned.1.call-start = ((), (), s32[]{:S(2)}) async-start(), calls=%async_computation.2 | async-start | bytes 20971520 | tf_op jit(solution)/shard_map/all_gather | solution.py:18
Sparse Core Ops, SparseCore 0:
  480.4 287.3 all-reduce.2
  795.5 105.9 all-gather.1
where the time goes:
time: 1330 us
  blocking collectives  741 us (56%)
  waiting for transfers between devices  392 us (29%)
  local copies, waits for them, and re-layouts  164 us (12%)
  between operations  14.7 us (1%)
  other arithmetic  13.9 us (1%)
    all_to_all x1, blocking collectives, on_device(): lax.all_to_all(local, 'fsdp', split_axis=2, concat_axis=1, tiled=True)  372 us
    all_to_all x1, blocking collectives, on_device(): lax.all_to_all(copies, 'fsdp', split_axis=1, concat_axis=2, tiled=True)  369 us
    unnamed x3, waiting for transfers between devices  286 us
    all_gather x1, waiting for transfers between devices, on_device(): copies = lax.all_gather(rounded, 'replica', axis=1, tiled=True)  106 us
    all_to_all x1, local copies, waits for them, and re-layouts, on_device(): lax.all_to_all(local, 'fsdp', split_axis=2, concat_axis=1, tiled=True)  60.3 us
    all_to_all x2, local copies, waits for them, and re-layouts, on_device(): lax.all_to_all(copies, 'fsdp', split_axis=1, concat_axis=2, tiled=True)  48.4 us
    unnamed x5, local copies, waits for them, and re-layouts  47 us
  transfers between devices with their start and end apart: 2, of which 2 were waited for; matrix products, arithmetic and copies ran while one was open for 0% of the time, Pallas kernels for 0%

commit v1 on v0

--- a/solution.py
+++ b/solution.py
@@ -15,7 +15,7 @@
     velocity = 0.9 * momentum + outer
     updated = master - 0.7 * (outer + 0.9 * velocity)
     rounded = updated.astype(jnp.bfloat16)
-    copies = lax.all_gather(rounded, "replica", axis=1, tiled=True)
+    copies = jnp.concatenate(lax.all_gather(rounded, "replica"), axis=1)
     spread = lax.all_to_all(copies, "fsdp", split_axis=1, concat_axis=2, tiled=True)
     return (updated, velocity, spread)
 

time: 1330 us -> 1200 us (0.902)
  waiting for transfers between devices: 392 us -> 230 us
  local copies, waits for them, and re-layouts: 164 us -> 195 us
    unnamed x3 -> x2, waiting for transfers between devices: 286 us -> 0.03 us
    reduce_scatter x0 -> x1, waiting for transfers between devices: none -> 124 us  [on_device(): lax.psum_scatter(moved.astype(jnp.float32).astype(jnp.bfloat16), 'replica...]
    reshape x0 -> x2, local copies, waits for them, and re-layouts: none -> 57.4 us  [on_device(): copies = jnp.concatenate(lax.all_gather(rounded, 'replica'), axis=1)]
    all_to_all x1, local copies, waits for them, and re-layouts: 60.3 us -> 40.8 us  [on_device(): lax.all_to_all(local, 'fsdp', split_axis=2, concat_axis=1, tiled=True)]
    unnamed x5 -> x2, local copies, waits for them, and re-layouts: 47 us -> 61.9 us
    all_to_all x2, local copies, waits for them, and re-layouts: 48.4 us -> 34.9 us  [on_device(): lax.all_to_all(copies, 'fsdp', split_axis=1, concat_axis=2, tiled=True)]
where the time goes in v1:
time: 1200 us; the launch traced here: 1190 us
  blocking collectives  741 us (62%)
  waiting for transfers between devices  230 us (19%)
  local copies, waits for them, and re-layouts  195 us (16%)
  between operations  14 us (1%)
  other arithmetic  13.3 us (1%)
    all_to_all x1, blocking collectives, on_device(): lax.all_to_all(local, 'fsdp', split_axis=2, concat_axis=1, tiled=True)  372 us
    all_to_all x1, blocking collectives, on_device(): lax.all_to_all(copies, 'fsdp', split_axis=1, concat_axis=2, tiled=True)  369 us
    reduce_scatter x1, waiting for transfers between devices, on_device(): lax.psum_scatter(moved.astype(jnp.float32).astype(jnp.bfloat16), 'replica...  124 us
    all_gather x1, waiting for transfers between devices, on_device(): copies = jnp.concatenate(lax.all_gather(rounded, 'replica'), axis=1)  106 us
    unnamed x2, local copies, waits for them, and re-layouts  61.9 us
    reshape x2, local copies, waits for them, and re-layouts, on_device(): copies = jnp.concatenate(lax.all_gather(rounded, 'replica'), axis=1)  57.4 us
    all_to_all x1, local copies, waits for them, and re-layouts, on_device(): lax.all_to_all(local, 'fsdp', split_axis=2, concat_axis=1, tiled=True)  40.8 us
    all_to_all x2, local copies, waits for them, and re-layouts, on_device(): lax.all_to_all(copies, 'fsdp', split_axis=1, concat_axis=2, tiled=True)  34.9 us
  transfers between devices with their start and end apart: 2, of which 2 were waited for; matrix products, arithmetic and copies ran while one was open for 0% of the time, Pallas kernels for 0%

profile of v1, /device:TPU:0, one launch (start us, length us, event | category | flops | bytes accessed | tf_op | source)
XLA Modules:
  0.0 1193.4 jit_solution(3925367726308313737)
XLA Ops:
  7.2 0.0 reduce-scatter.2.cloned.1.call-start
  7.2 40.8 %copy.12 = bf16[1,2,256,16384]{2,1,3,0:T(2,128)(2,1)} copy(bf16[1,2,256,16384]{3,2,1,0:T(8,128)(2,1)} %param.3) | data formatting | bytes 33554432 | tf_op args[0]
  48.0 372.0 %all_to_all.36 = bf16[2,256,16384]{1,0,2:T(2,128)(2,1)} all-to-all(bf16[2,256,16384]{1,0,2:T(2,128)(2,1)} %bitcast.18), channel_id=1, replica_groups=mesh['replica'=4,'fsdp'=8] {'fsdp'}, dimensions={2} | all-to-all | bytes 33554432 | tf_op jit(solution)/shard_map/all_to_all | solution.py:10
  420.0 40.8 %copy.13 = bf16[2,8,256,2048]{3,2,1,0:T(8,128)(2,1)} copy(bf16[2,8,256,2048]{2,0,3,1:T(2,128)(2,1)} %bitcast.14) | data formatting | bytes 33554432 | tf_op jit(solution)/shard_map/all_to_all | solution.py:10
  460.8 0.0 reduce-scatter.2.cloned.1.call-update
  460.8 0.0 all-gather.3.cloned.1.call-start
  460.9 124.2 %reduce-scatter.2.cloned.1.call-done = bf16[2,512,2048]{2,1,0:T(8,128)(2,1)} async-done(((bf16[2,2048,2048]{2,1,0:T(8,128)(2,1)}), bf16[2,512,2048]{2,1,0:T(8,128)(2,1)}) %reduce-scatter.2.cloned.1.call-update) | async-done | bytes 4194320 | tf_op jit(solution)/shard_map/reduce_scatter | solution.py:11
  585.0 13.3 %fusion = (bf16[2,512,2048]{2,1,0:T(8,128)(2,1)}, f32[2,512,2048]{2,1,0:T(8,128)}, f32[2,512,2048]{2,1,0:T(8,128)}) fusion(f32[2,512,2048]{2,1,0:T(8,128)} %param.4, bf16[2,512,2048]{2,1,0:T(8,128)(2,1)} %reduce-scatter.2.cloned.1.call-done, f32[2,512,2048]{2,1,0:T(8,128)} %param.5), kind=kLoop, calls=%fused_computation.3 | loop fusion | flops 18874368 | bytes 41943040 | tf_op jit(solution)/shard_map/convert_element_type | solution.py:17
  598.3 0.0 all-gather.3.cloned.1.call-update
  598.3 106.0 %all-gather.3.cloned.1.call-done = bf16[8,512,2048]{2,1,0:T(8,128)(2,1)} async-done(((bf16[2,512,2048]{2,1,0:T(8,128)(2,1)}), bf16[8,512,2048]{2,1,0:T(8,128)(2,1)}) %all-gather.3.cloned.1.call-update) | async-done | bytes 16777232 | tf_op jit(solution)/shard_map/all_gather | solution.py:18
  704.4 8.5 copy.14
  712.9 48.9 %copy.15 = bf16[2,2048,2048]{2,0,1:T(2,128)(2,1)} copy(bf16[2,2048,2048]{2,1,0:T(8,128)(2,1)S(1)} %bitcast.15) | data formatting | bytes 33554432 | tf_op jit(solution)/shard_map/reshape | solution.py:18
  761.8 368.7 %all_to_all.37 = bf16[2,2048,2048]{2,0,1:T(2,128)(2,1)S(1)} all-to-all(bf16[2,2048,2048]{2,0,1:T(2,128)(2,1)} %copy.15), channel_id=1, replica_groups=mesh['replica'=4,'fsdp'=8] {'fsdp'}, dimensions={1} | all-to-all | bytes 33554432 | tf_op jit(solution)/shard_map/all_to_all | solution.py:19
  1130.5 13.3 %copy.16 = bf16[2,2048,2048]{2,1,0:T(8,128)(2,1)} copy(bf16[2,2048,2048]{2,0,1:T(2,128)(2,1)S(1)} %all_to_all.37) | data formatting | bytes 33554432 | tf_op jit(solution)/shard_map/all_to_all | solution.py:19
  1143.8 21.5 %copy.17 = bf16[2,256,8,2048]{1,3,2,0:T(8,128)(2,1)} copy(bf16[2,256,8,2048]{3,1,2,0:T(8,128)(2,1)} %bitcast.16) | data formatting | bytes 33554432 | tf_op jit(solution)/shard_map/all_to_all | solution.py:19
  1165.3 21.2 %copy.18 = bf16[2,256,16384]{2,1,0:T(8,128)(2,1)} copy(bf16[2,256,16384]{1,2,0:T(8,128)(2,1)} %bitcast.17) | data formatting | bytes 33554432
Async XLA Ops:
  7.2 577.9 %reduce-scatter.2.cloned.1.call-start = ((), (), s32[]{:S(2)}) async-start(), calls=%async_computation.3 | async-start | bytes 20971520 | tf_op jit(solution)/shard_map/reduce_scatter | solution.py:11
  460.8 243.6 %all-gather.3.cloned.1.call-start = ((), (), s32[]{:S(2)}) async-start(), calls=%async_computation.4 | async-start | bytes 20971520 | tf_op jit(solution)/shard_map/all_gather | solution.py:18
Sparse Core Ops, SparseCore 0:
  460.9 124.0 reduce-scatter.1
  598.5 105.8 all-gather.2
